TPU v7x, 32 devices: a whole 2x2x4 slice. The times are simulated.
32 devices in a mesh: ctx: 2 (over x), tp: 4 (over y, core), dp: 4 (over z).
Axes of the slice: x: 2, y: 2, z: 4, core: 2. Of those that a mesh axis runs over, the one named last changes fastest.
Arguments:
- hidden: bfloat16 [4, 1024, 4096], P('dp', 'ctx', 'tp'), may hold values from -6 to 6
- target: bfloat16 [4, 1024, 4096], P('dp', 'ctx', 'tp'), may hold values from -24 to 24
- gain: float32 [4096], replicated, may hold values from 0.5 to 1.5
- w_query: bfloat16 [4096, 2048], P(('ctx', 'dp'), 'tp'), may hold values from -2.15625 to 2.15625
- w_key: bfloat16 [4096, 512], P(('ctx', 'dp'), 'tp'), may hold values from -0.09375 to 0.09375
- value_matrix: bfloat16 [4096, 512], P(('ctx', 'dp'), 'tp'), may hold values from -0.09375 to 0.09375
- w_out: bfloat16 [2048, 4096], P('tp', ('ctx', 'dp')), may hold values from -0.125 to 0.125
- block_order: int32 [4], replicated, may hold values from 0 to 3, each once
Outputs:
- branch: bfloat16 [4, 1024, 4096], P('dp', 'ctx', 'tp')
- loss: float32 [], replicated
Inputs may be any that keep to these rules, and one draw needn't show every extreme that they name: block_order is a permutation of 0 to 3.
All inputs are finite; a program needn't handle non-finite values.
Results may differ from a plain program's by a relative error of at most 0.013.
The roundings to bfloat16 on the way count: a program that leaves them out, or rounds other values in their place, can miss the bound.
Values may be sent and summed in bfloat16 or wider, within the bound.
A program may use at most 128 MiB of HBM per device.

v0:
```python
import jax
import jax.numpy as jnp
from jax import lax
from jax.sharding import PartitionSpec as P

MODEL_WIDTH = 4096
QUERY_HEADS = 16
KEY_VALUE_HEADS = 4
HEAD_SIZE = 128
rope_base = 500000.0


def shifted(value, axis, by):
    peers = lax.axis_size(axis)
    return lax.ppermute(value, axis, [(i, (i + by) % peers) for i in range(peers)])


def positions(order, start, rows, half):
    index = start + lax.iota(jnp.int32, rows)
    block = index // half
    slots = lax.iota(jnp.int32, order.shape[0])
    chosen = jnp.sum(jnp.where(block[:, None] == slots[None, :], order[None, :], 0), axis=1)
    return chosen * half + index % half


def apply_rotary(values, token_places):
    half = values.shape[-1] // 2
    freqs = rope_base ** (-(jnp.arange(half, dtype=jnp.float32) * 2.0) / values.shape[-1])
    angles = token_places.astype(jnp.float32)[:, None] * freqs[None, :]
    cosine = jnp.cos(angles)[:, None, :]
    sine = jnp.sin(angles)[:, None, :]
    first = values[..., :half]
    second = values[..., half:]
    return jnp.concatenate(
        [first * cosine - second * sine, second * cosine + first * sine], axis=-1
    )


def attend(state, query_rows, qpos, piece, kpos):
    peak, total, accum = state
    rows = piece.shape[1]
    local_heads = query_rows.shape[1]
    pair = piece.reshape(2, rows, local_heads, HEAD_SIZE)
    scores = jnp.einsum(
        "qcgd,kcd->cgqk", query_rows, pair[0], preferred_element_type=jnp.float32
    ) * (1.0 / HEAD_SIZE**0.5)
    allowed = (qpos[:, None] >= kpos[None, :])[None, None]
    scores = jnp.where(allowed, scores, -1e30)
    new_peak = jnp.maximum(peak, jnp.max(scores, axis=-1))
    weights = jnp.where(allowed, jnp.exp(scores - new_peak[..., None]), 0.0)
    factor = jnp.exp(peak - new_peak)
    total = total * factor + jnp.sum(weights, axis=-1)
    update = jnp.einsum(
        "cgqk,kcd->qcgd", weights.astype(jnp.bfloat16), pair[1], preferred_element_type=jnp.float32
    )
    accum = accum * jnp.transpose(factor, (2, 0, 1))[..., None] + update
    return (new_peak, total, accum)


def on_device(hidden, target, gain, w_query, w_key, value_matrix, w_out, block_order):
    rows = hidden.shape[1]
    half = rows // 2
    local = hidden[0]
    whole = lax.all_gather(local, "tp", axis=1, tiled=True)
    wide = whole.astype(jnp.float32)
    normed = (
        wide * lax.rsqrt(jnp.mean(wide * wide, axis=1, keepdims=True) + 1e-05) * gain[None, :]
    ).astype(jnp.bfloat16)
    pieces = (
        lax.all_gather(w_query, ("ctx", "dp"), axis=0, tiled=True),
        lax.all_gather(w_key, ("ctx", "dp"), axis=0, tiled=True),
        lax.all_gather(value_matrix, ("ctx", "dp"), axis=0, tiled=True),
    )
    query_rows, key, value_rows = tuple(
        (jnp.dot(normed, piece, preferred_element_type=jnp.float32) for piece in pieces)
    )
    shard = lax.axis_index("ctx")
    qpos = positions(block_order, shard * rows, rows, half)
    local_heads = w_key.shape[1] // HEAD_SIZE
    query_group = QUERY_HEADS // KEY_VALUE_HEADS
    query_rows = (
        apply_rotary(query_rows.reshape(rows, local_heads * query_group, HEAD_SIZE), qpos)
        .astype(jnp.bfloat16)
        .reshape(rows, local_heads, query_group, HEAD_SIZE)
    )
    key = (
        apply_rotary(key.reshape(rows, local_heads, HEAD_SIZE), qpos)
        .astype(jnp.bfloat16)
        .reshape(rows, local_heads * HEAD_SIZE)
    )
    pair = jnp.stack([key, value_rows.astype(jnp.bfloat16)])
    state = (
        jnp.full((local_heads, query_group, rows), -1e30, jnp.float32),
        jnp.zeros((local_heads, query_group, rows), jnp.float32),
        jnp.zeros((rows, local_heads, query_group, HEAD_SIZE), jnp.float32),
    )
    count = lax.axis_size("ctx")
    state = attend(state, query_rows, qpos, pair, qpos)

    def turn(step, carry):
        moved, inner = carry
        moved = shifted(moved, "ctx", 1)
        source = (shard - step) % count
        return (
            moved,
            attend(
                inner, query_rows, qpos, moved, positions(block_order, source * rows, rows, half)
            ),
        )

    moved_end, state = lax.fori_loop(1, count, turn, (pair, state))
    peak, total, accum = state
    attn = (
        (accum / jnp.transpose(total, (2, 0, 1))[..., None])
        .astype(jnp.bfloat16)
        .reshape(rows, local_heads * query_group * HEAD_SIZE)
    )
    terms = jnp.dot(
        attn,
        lax.all_gather(w_out, ("ctx", "dp"), axis=1, tiled=True),
        preferred_element_type=jnp.float32,
    )
    summed = lax.psum_scatter(terms.astype(jnp.bfloat16), "tp", scatter_dimension=1, tiled=True)
    resid = local.astype(jnp.float32) + summed.astype(jnp.float32) - target[0].astype(jnp.float32)
    squares = lax.psum(jnp.sum(resid * resid), ("ctx", "tp", "dp"))
    loss = squares / (lax.axis_size("dp") * lax.axis_size("ctx") * rows * MODEL_WIDTH)
    return (summed[None], loss)


def solution(mesh):
    in_specs = (
        P("dp", "ctx", "tp"),
        P("dp", "ctx", "tp"),
        P(),
        P(("ctx", "dp"), "tp"),
        P(("ctx", "dp"), "tp"),
        P(("ctx", "dp"), "tp"),
        P("tp", ("ctx", "dp")),
        P(),
    )
    out_specs = (P("dp", "ctx", "tp"), P())
    return jax.shard_map(
        on_device, mesh=mesh, in_specs=in_specs, out_specs=out_specs, check_vma=False
    )
```

profile of v0, /device:TPU:0, one launch (start us, length us, event | category | flops | bytes accessed | tf_op | source)
XLA Modules:
  0.0 378.8 jit_solution(6131819200116777629)
XLA Ops:
  7.2 0.7 all-gather.15.cloned.1.call-update
  8.0 0.7 all-gather.7.cloned.1.call-update
  8.7 0.7 all-gather.11.cloned.1.call-update
  9.4 0.5 all-gather.9.cloned.1.call-update
  10.0 0.5 all-gather.13.cloned.1.call-update
  10.7 0.7 select_reduce_fusion
  11.4 1.8 multiply_cosine_fusion
  13.2 0.4 broadcast_compare_fusion
  13.6 33.2 %all-gather.15.cloned.1.call-done = bf16[1,512,4096]{2,1,0:T(8,128)(2,1)} async-done(((bf16[1,512,1024]{2,1,0:T(8,128)(2,1)}), bf16[1,512,4096]{2,1,0:T(8,128)(2,1)}) %all-gather.15.cloned.1.call-update) | async-done | bytes 4194320 | tf_op jit(solution)/shard_map/all_gather | solution.py:64
  46.8 3.1 fusion
  49.9 39.3 %all-gather.7.cloned.1.call-done = bf16[4096,128]{1,0:T(8,128)(2,1)} async-done(((bf16[512,128]{1,0:T(8,128)(2,1)}), bf16[4096,128]{1,0:T(8,128)(2,1)}) %all-gather.7.cloned.1.call-update) | async-done | bytes 1048592 | tf_op jit(solution)/shard_map/all_gather | solution.py:71
  89.2 4.1 %convolution_bitcast_fusion = f32[512,1,128]{0,2,1:T(8,128)S(1)} fusion(bf16[4096,128]{1,0:T(8,128)(2,1)} %all-gather.7.cloned.1.call-done, bf16[1,512,4096]{2,1,0:T(8,128)(2,1)} %all-gather.15.cloned.1.call-done, f32[4096]{0:T(1024)S(1)} %copy-done.4, f32[512]{0:T(512)S(1)} %add_rsqrt_fusion), kind=kOutput, calls=%fused_computation.31 | convolution fusion | flops 545259520 | bytes 5523456 | tf_op jit(solution)/shard_map/dot_general | solution.py:75
  93.3 0.6 fusion.41
  93.9 36.5 %all-gather.11.cloned.1.call-done = bf16[4096,128]{1,0:T(8,128)(2,1)} async-done(((bf16[512,128]{1,0:T(8,128)(2,1)}), bf16[4096,128]{1,0:T(8,128)(2,1)}) %all-gather.11.cloned.1.call-update) | async-done | bytes 1048592 | tf_op jit(solution)/shard_map/all_gather | solution.py:72
  130.4 4.1 %convolution_convert_fusion.1 = bf16[512,128]{0,1:T(8,128)(2,1)S(1)} fusion(bf16[4096,128]{1,0:T(8,128)(2,1)} %all-gather.11.cloned.1.call-done, bf16[1,512,4096]{2,1,0:T(8,128)(2,1)} %all-gather.15.cloned.1.call-done, f32[4096]{0:T(1024)S(1)} %copy-done.4, f32[512]{0:T(512)S(1)} %add_rsqrt_fusion), kind=kOutput, calls=%fused_computation.32 | convolution fusion | flops 545325056 | bytes 5392384 | tf_op jit(solution)/shard_map/dot_general | solution.py:75
  134.5 0.8 pad_maximum_fusion.1
  135.3 0.6 collective-permute-start
  135.9 68.1 %all-gather.9.cloned.1.call-done = bf16[4096,512]{1,0:T(8,128)(2,1)} async-done(((bf16[512,512]{1,0:T(8,128)(2,1)}), bf16[4096,512]{1,0:T(8,128)(2,1)}) %all-gather.9.cloned.1.call-update) | async-done | bytes 4194320 | tf_op jit(solution)/shard_map/all_gather | solution.py:70
  203.9 5.9 %fusion.74 = f32[512,512]{0,1:T(8,128)S(1)} fusion(bf16[4096,512]{1,0:T(8,128)(2,1)} %all-gather.9.cloned.1.call-done, bf16[1,512,4096]{2,1,0:T(8,128)(2,1)} %all-gather.15.cloned.1.call-done, f32[4096]{0:T(1024)S(1)} %copy-done.4, f32[512]{0:T(512)S(1)} %add_rsqrt_fusion), kind=kOutput, calls=%fused_computation.109 | convolution fusion | flops 2155872256 | bytes 9455616 | tf_op jit(solution)/shard_map/dot_general | solution.py:75
  210.3 0.3 copy.32
  210.6 1.2 subtract_convert_fusion
  211.9 1.2 fusion.3
  213.1 2.1 fusion.4
  215.3 1.0 fusion.5
  216.3 1.2 fusion.7
  217.6 1.3 fusion.28
  218.9 2.2 divide_convert_fusion
  221.1 57.8 %all-gather.13.cloned.1.call-done = bf16[512,4096]{1,0:T(8,128)(2,1)} async-done(((bf16[512,512]{1,0:T(8,128)(2,1)}), bf16[512,4096]{1,0:T(8,128)(2,1)}) %all-gather.13.cloned.1.call-update) | async-done | bytes 4194320 | tf_op jit(solution)/shard_map/all_gather | solution.py:120
  279.0 6.5 %convolution_convert_fusion = bf16[512,4096]{1,0:T(8,128)(2,1)} fusion(bf16[512,512]{0,1:T(8,128)(2,1)S(1)} %bitcast.172, bf16[512,4096]{1,0:T(8,128)(2,1)} %all-gather.13.cloned.1.call-done), kind=kOutput, calls=%fused_computation.5 | convolution fusion | flops 2149580800 | bytes 8912896 | tf_op jit(solution)/shard_map/dot_general | solution.py:118
  285.6 42.7 %reduce-scatter.2.cloned.1.call-done = bf16[512,1024]{1,0:T(8,128)(2,1)} async-done(((bf16[512,4096]{1,0:T(8,128)(2,1)}), bf16[512,1024]{1,0:T(8,128)(2,1)}) %reduce-scatter.2.cloned.1.call-update) | async-done | bytes 1048592 | tf_op jit(solution)/shard_map/reduce_scatter | solution.py:123
  328.3 2.4 fusion.12
  330.7 39.5 %psum.7 = f32[]{:T(128)} all-reduce(f32[]{:T(128)} %fusion.12), channel_id=1, replica_groups=mesh['ctx'=2,'tp'=4,'dp'=4] {'ctx','tp','dp'}, use_global_device_ids=true, to_apply=%region_9.10 | all-reduce | flops 1 | bytes 8 | tf_op jit(solution)/shard_map/psum | solution.py:125
  (27 shorter events, 0.8 us)
Async XLA Ops:
  7.2 82.0 %copy-start.4 = (f32[4096]{0:T(1024)S(1)}, f32[4096]{0:T(1024)}, u32[]{:S(2)}) copy-start(f32[4096]{0:T(1024)} %param.10) | copy-start | bytes 49156
  7.2 39.6 %all-gather.15.cloned.1.call-start = ((), (), s32[]{:S(2)}) async-start(), calls=%async_computation.6 | async-start | bytes 5242880 | tf_op jit(solution)/shard_map/all_gather | solution.py:64
  7.9 81.3 %all-gather.7.cloned.1.call-start = ((), (), s32[]{:S(2)}) async-start(), calls=%async_computation.1 | async-start | bytes 1179648 | tf_op jit(solution)/shard_map/all_gather | solution.py:71
  8.7 121.8 %all-gather.11.cloned.1.call-start = ((), (), s32[]{:S(2)}) async-start(), calls=%async_computation.3 | async-start | bytes 1179648 | tf_op jit(solution)/shard_map/all_gather | solution.py:72
  9.4 194.5 %all-gather.9.cloned.1.call-start = ((), (), s32[]{:S(2)}) async-start(), calls=%async_computation.2 | async-start | bytes 4718592 | tf_op jit(solution)/shard_map/all_gather | solution.py:70
  10.0 269.0 %all-gather.13.cloned.1.call-start = ((), (), s32[]{:S(2)}) async-start(), calls=%async_computation.4 | async-start | bytes 4718592 | tf_op jit(solution)/shard_map/all_gather | solution.py:120
  10.6 317.7 %reduce-scatter.2.cloned.1.call-start = ((), (), s32[]{:S(2)}) async-start(), calls=%async_computation.5 | async-start | bytes 5242880 | tf_op jit(solution)/shard_map/reduce_scatter | solution.py:123
  134.5 1.4 copy-start.2
  135.3 77.8 %collective-permute-start = (bf16[2,512,128]{1,2,0:T(8,128)(2,1)}, bf16[2,512,128]{1,2,0:T(8,128)(2,1)}, u32[]{:S(2)}, u32[]{:S(2)}) collective-permute-start(bf16[2,512,128]{1,2,0:T(8,128)(2,1)} %pad_maximum_fusion.1), channel_id=1, source_target_pairs={{0,16},{16,0},{1,17},{17,1},{2,18},{18,2},{3,19},{19,3},{4,20},{20... | collective-permute-start | bytes 786440 | tf_op jit(solution)/shard_map/while/body/eval_jaxpr/ppermute | solution.py:15
  215.2 2.3 copy-start.3
  285.5 42.8 %copy-start = (bf16[1,512,1024]{2,1,0:T(8,128)(2,1)S(1)}, bf16[1,512,1024]{2,1,0:T(8,128)(2,1)}, u32[]{:S(2)}) copy-start(bf16[1,512,1024]{2,1,0:T(8,128)(2,1)} %param.8) | copy-start | bytes 3145732
  285.5 42.8 %copy-start.1 = (bf16[1,512,1024]{2,1,0:T(8,128)(2,1)S(1)}, bf16[1,512,1024]{2,1,0:T(8,128)(2,1)}, u32[]{:S(2)}) copy-start(bf16[1,512,1024]{2,1,0:T(8,128)(2,1)} %param.9) | copy-start | bytes 3145732
Sparse Core Ops, SparseCore 0:
  9.5 37.1 all-gather.14
  48.9 40.2 all-gather.6
  91.3 39.0 all-gather.10
  132.4 71.5 all-gather.8
  205.8 73.1 all-gather.12
  285.7 42.5 reduce-scatter.1
where the time goes:
time: 379 us
  waiting for transfers between devices  281 us (74%)
  blocking collectives  39.5 us (10%)
  matrix products  27.6 us (7%)
  between operations  16.1 us (4%)
  other arithmetic  13.3 us (4%)
    all_gather x1, waiting for transfers between devices, on_device(): lax.all_gather(w_query, ('ctx', 'dp'), axis=0, tiled=True)  68.1 us
    all_gather x1, waiting for transfers between devices, on_device(): lax.all_gather(w_out, ('ctx', 'dp'), axis=1, tiled=True)  57.8 us
    reduce_scatter x1, waiting for transfers between devices, on_device(): lax.psum_scatter(terms.astype(jnp.bfloat16), 'tp', scatter_dimension=1, t...  42.7 us
    psum x1, blocking collectives, on_device(): squares = lax.psum(jnp.sum(resid * resid), ('ctx', 'tp', 'dp'))  39.5 us
    all_gather x1, waiting for transfers between devices, on_device(): lax.all_gather(w_key, ('ctx', 'dp'), axis=0, tiled=True)  39.3 us
    all_gather x1, waiting for transfers between devices, on_device(): lax.all_gather(value_matrix, ('ctx', 'dp'), axis=0, tiled=True)  36.5 us
    all_gather x1, waiting for transfers between devices, on_device(): whole = lax.all_gather(local, 'tp', axis=1, tiled=True)  33.2 us
    dot_general x3, matrix products, on_device(): jnp.dot(normed, piece, preferred_element_type=jnp.float32)  14.1 us
  transfers between devices with their start and end apart: 7, of which 6 were waited for; matrix products, arithmetic and copies ran while one was open for 9% of the time, Pallas kernels for 0%

commit v1 on v0

--- a/solution.py
+++ b/solution.py
@@ -8,6 +8,16 @@
 KEY_VALUE_HEADS = 4
 HEAD_SIZE = 128
 rope_base = 500000.0
+
+
+def turned_line(x, mesh_axis, d):
+    size = lax.axis_size(mesh_axis)
+    held, blocks = (x, [x])
+    for _ in range(size - 1):
+        held = lax.ppermute(held, mesh_axis, [(i, (i + 1) % size) for i in range(size)])
+        blocks.insert(0, held)
+    merged = jnp.concatenate(blocks, axis=d)
+    return jnp.roll(merged, (lax.axis_index(mesh_axis) + 1) * x.shape[d], axis=d)
 
 
 def shifted(value, axis, by):
@@ -61,7 +71,7 @@
     rows = hidden.shape[1]
     half = rows // 2
     local = hidden[0]
-    whole = lax.all_gather(local, "tp", axis=1, tiled=True)
+    whole = turned_line(local, "tp", 1)
     wide = whole.astype(jnp.float32)
     normed = (
         wide * lax.rsqrt(jnp.mean(wide * wide, axis=1, keepdims=True) + 1e-05) * gain[None, :]

time: 379 us -> 343 us (0.905)
  waiting for transfers between devices: 281 us -> 236 us
  local copies, waits for them, and re-layouts: 0.75 us -> 9.67 us
    ppermute x0 -> x3, waiting for transfers between devices: none -> 39.4 us  [turned_line(): lax.ppermute(held, mesh_axis, [(i, (i + 1) % size) for i in range(size)])]
    all_gather x1, waiting for transfers between devices: 39.3 us -> 0.02 us  [on_device(): lax.all_gather(w_key, ('ctx', 'dp'), axis=0, tiled=True)]
    all_gather x1 -> x0, waiting for transfers between devices: 33.2 us -> none  [on_device(): whole = lax.all_gather(local, 'tp', axis=1, tiled=True)]
    unnamed x12 -> x23, local copies, waits for them, and re-layouts: 0.68 us -> 8.7 us
    all_gather x1, waiting for transfers between devices: 36.5 us -> 28.9 us  [on_device(): lax.all_gather(value_matrix, ('ctx', 'dp'), axis=0, tiled=True)]
  transfers between devices with their start and end apart: 7 -> 9, of which waited for: 6 -> 7; matrix products, arithmetic and copies ran while one was open for 9% -> 11% of each run, Pallas kernels for 0% -> 0%
where the time goes in v1:
time: 343 us; the launch traced here: 342 us
  waiting for transfers between devices  236 us (69%)
  blocking collectives  39.5 us (12%)
  matrix products  28.6 us (8%)
  between operations  15.9 us (5%)
  other arithmetic  11.8 us (3%)
  local copies, waits for them, and re-layouts  9.67 us (3%)
    all_gather x1, waiting for transfers between devices, on_device(): lax.all_gather(w_query, ('ctx', 'dp'), axis=0, tiled=True)  67.6 us
    all_gather x1, waiting for transfers between devices, on_device(): lax.all_gather(w_out, ('ctx', 'dp'), axis=1, tiled=True)  54.9 us
    reduce_scatter x1, waiting for transfers between devices, on_device(): lax.psum_scatter(terms.astype(jnp.bfloat16), 'tp', scatter_dimension=1, t...  42.7 us
    psum x1, blocking collectives, on_device(): squares = lax.psum(jnp.sum(resid * resid), ('ctx', 'tp', 'dp'))  39.5 us
    ppermute x3, waiting for transfers between devices, turned_line(): lax.ppermute(held, mesh_axis, [(i, (i + 1) % size) for i in range(size)])  39.4 us
    all_gather x1, waiting for transfers between devices, on_device(): lax.all_gather(value_matrix, ('ctx', 'dp'), axis=0, tiled=True)  28.9 us
    dot_general x3, matrix products, on_device(): jnp.dot(normed, piece, preferred_element_type=jnp.float32)  14.2 us
    unnamed x23, local copies, waits for them, and re-layouts  8.7 us
  transfers between devices with their start and end apart: 9, of which 7 were waited for; matrix products, arithmetic and copies ran while one was open for 11% of the time, Pallas kernels for 0%

profile of v1, /device:TPU:0, one launch (start us, length us, event | category | flops | bytes accessed | tf_op | source)
XLA Modules:
  0.0 342.5 jit_solution(18265280814586790945)
XLA Ops:
  7.9 0.7 all-gather.9.cloned.1.call-update
  8.7 0.7 all-gather.7.cloned.1.call-update
  10.0 14.6 %collective-permute-done = bf16[512,1024]{1,0:T(8,128)(2,1)S(1)} collective-permute-done((bf16[512,1024]{1,0:T(8,128)(2,1)}, bf16[512,1024]{1,0:T(8,128)(2,1)S(1)}, u32[]{:S(2)}, u32[]{:S(2)}) %collective-permute-start) | collective-permute-done | bytes 1048608 | tf_op jit(solution)/shard_map/ppermute | solution.py:17
  24.8 14.1 %collective-permute-done.1 = bf16[512,1024]{1,0:T(8,128)(2,1)S(1)} collective-permute-done((bf16[512,1024]{1,0:T(8,128)(2,1)S(1)}, bf16[512,1024]{1,0:T(8,128)(2,1)S(1)}, u32[]{:S(2)}, u32[]{:S(2)}) %collective-permute-start.1) | collective-permute-done | bytes 1048608 | tf_op jit(solution)/shard_map/ppermute | solution.py:17
  38.9 0.7 select_reduce_fusion
  39.6 1.8 multiply_cosine_fusion
  41.5 1.0 broadcast_compare_fusion
  42.5 10.7 %collective-permute-done.2 = bf16[512,1024]{1,0:T(8,128)(2,1)} collective-permute-done((bf16[512,1024]{1,0:T(8,128)(2,1)S(1)}, bf16[512,1024]{1,0:T(8,128)(2,1)}, u32[]{:S(2)}, u32[]{:S(2)}) %collective-permute-start.2) | collective-permute-done | bytes 1048608 | tf_op jit(solution)/shard_map/ppermute | solution.py:17
  53.2 1.3 constant_dynamic-update-slice_fusion.7
  54.8 1.3 constant_dynamic-update-slice_fusion.3
  56.4 3.2 copy-done.1
  59.6 0.9 fusion
  60.6 4.2 %convolution_bitcast_fusion = f32[512,1,128]{0,2,1:T(8,128)S(1)} fusion(bf16[4096,128]{1,0:T(8,128)(2,1)} %all-gather.5.cloned.1.call-done, f32[4096]{0:T(1024)S(1)} %copy-done.6, f32[512]{0:T(512)S(1)} %add_rsqrt_fusion, bf16[512,8192]{1,0:T(8,128)(2,1)} %copy-done.1, s32[]{:T(128)S(6)} %select_n.92), kind=kOutput, calls=%fused_computation.30 | convolution fusion | flops 545259520 | bytes 5523460 | tf_op jit(solution)/shard_map/dot_general | solution.py:85
  65.4 28.9 %all-gather.9.cloned.1.call-done = bf16[4096,128]{1,0:T(8,128)(2,1)} async-done(((bf16[512,128]{1,0:T(8,128)(2,1)}), bf16[4096,128]{1,0:T(8,128)(2,1)}) %all-gather.9.cloned.1.call-update) | async-done | bytes 1048592 | tf_op jit(solution)/shard_map/all_gather | solution.py:82
  94.3 4.1 %convolution_convert_fusion.1 = bf16[512,128]{0,1:T(8,128)(2,1)S(1)} fusion(bf16[4096,128]{1,0:T(8,128)(2,1)} %all-gather.9.cloned.1.call-done, f32[4096]{0:T(1024)S(1)} %copy-done.6, f32[512]{0:T(512)S(1)} %add_rsqrt_fusion, bf16[512,8192]{1,0:T(8,128)(2,1)} %copy-done.1, s32[]{:T(128)S(6)} %select_n.92), kind=kOutput, calls=%fused_computation.31 | convolution fusion | flops 545325056 | bytes 5392388 | tf_op jit(solution)/shard_map/dot_general | solution.py:85
  99.0 0.7 pad_maximum_fusion.1
  100.4 67.6 %all-gather.7.cloned.1.call-done = bf16[4096,512]{1,0:T(8,128)(2,1)} async-done(((bf16[512,512]{1,0:T(8,128)(2,1)}), bf16[4096,512]{1,0:T(8,128)(2,1)}) %all-gather.7.cloned.1.call-update) | async-done | bytes 4194320 | tf_op jit(solution)/shard_map/all_gather | solution.py:80
  168.0 5.9 %fusion.74 = f32[512,512]{0,1:T(8,128)S(1)} fusion(bf16[4096,512]{1,0:T(8,128)(2,1)} %all-gather.7.cloned.1.call-done, f32[4096]{0:T(1024)S(1)} %copy-done.6, f32[512]{0:T(512)S(1)} %add_rsqrt_fusion, bf16[512,8192]{1,0:T(8,128)(2,1)} %copy-done.1, s32[]{:T(128)S(6)} %select_n.92), kind=kOutput, calls=%fused_computation.116 | convolution fusion | flops 2155872256 | bytes 9455620 | tf_op jit(solution)/shard_map/dot_general | solution.py:85
  173.9 0.9 fusion.79
  175.2 1.4 copy.32
  176.6 1.3 subtract_convert_fusion
  177.9 2.2 fusion.3
  180.1 2.1 fusion.4
  182.3 1.1 fusion.5
  183.3 1.2 fusion.7
  184.6 1.3 fusion.28
  185.9 2.2 divide_convert_fusion
  188.2 54.9 %all-gather.11.cloned.1.call-done = bf16[512,4096]{1,0:T(8,128)(2,1)} async-done(((bf16[512,512]{1,0:T(8,128)(2,1)}), bf16[512,4096]{1,0:T(8,128)(2,1)}) %all-gather.11.cloned.1.call-update) | async-done | bytes 4194320 | tf_op jit(solution)/shard_map/all_gather | solution.py:130
  243.1 6.5 %convolution_convert_fusion = bf16[512,4096]{1,0:T(8,128)(2,1)} fusion(bf16[512,512]{0,1:T(8,128)(2,1)S(1)} %bitcast.167, bf16[512,4096]{1,0:T(8,128)(2,1)} %all-gather.11.cloned.1.call-done), kind=kOutput, calls=%fused_computation.5 | convolution fusion | flops 2149580800 | bytes 8912896 | tf_op jit(solution)/shard_map/dot_general | solution.py:128
  249.6 42.7 %reduce-scatter.2.cloned.1.call-done = bf16[512,1024]{1,0:T(8,128)(2,1)} async-done(((bf16[512,4096]{1,0:T(8,128)(2,1)}), bf16[512,1024]{1,0:T(8,128)(2,1)}) %reduce-scatter.2.cloned.1.call-update) | async-done | bytes 1048592 | tf_op jit(solution)/shard_map/reduce_scatter | solution.py:133
  292.3 2.4 fusion.12
  294.7 39.5 %psum.7 = f32[]{:T(128)} all-reduce(f32[]{:T(128)} %fusion.12), channel_id=1, replica_groups=mesh['ctx'=2,'tp'=4,'dp'=4] {'ctx','tp','dp'}, use_global_device_ids=true, to_apply=%region_9.10 | all-reduce | flops 1 | bytes 8 | tf_op jit(solution)/shard_map/psum | solution.py:135
  (42 shorter events, 4.3 us)
Async XLA Ops:
  7.2 53.4 %all-gather.5.cloned.1.call-start = ((), (), s32[]{:S(2)}) async-start(), calls=%async_computation.1 | async-start | bytes 1179648 | tf_op jit(solution)/shard_map/all_gather | solution.py:81
  7.9 86.4 %all-gather.9.cloned.1.call-start = ((), (), s32[]{:S(2)}) async-start(), calls=%async_computation.3 | async-start | bytes 1179648 | tf_op jit(solution)/shard_map/all_gather | solution.py:82
  8.6 46.0 %copy-start = (bf16[1,512,1024]{2,1,0:T(8,128)(2,1)S(1)}, bf16[1,512,1024]{2,1,0:T(8,128)(2,1)}, u32[]{:S(2)}) copy-start(bf16[1,512,1024]{2,1,0:T(8,128)(2,1)} %param.8) | copy-start | bytes 3145732
  8.7 159.3 %all-gather.7.cloned.1.call-start = ((), (), s32[]{:S(2)}) async-start(), calls=%async_computation.2 | async-start | bytes 4718592 | tf_op jit(solution)/shard_map/all_gather | solution.py:80
  9.4 233.7 %all-gather.11.cloned.1.call-start = ((), (), s32[]{:S(2)}) async-start(), calls=%async_computation.4 | async-start | bytes 4718592 | tf_op jit(solution)/shard_map/all_gather | solution.py:130
  9.4 15.2 %collective-permute-start = (bf16[512,1024]{1,0:T(8,128)(2,1)}, bf16[512,1024]{1,0:T(8,128)(2,1)S(1)}, u32[]{:S(2)}, u32[]{:S(2)}) collective-permute-start(bf16[512,1024]{1,0:T(8,128)(2,1)} %bitcast.160), channel_id=1, source_target_pairs={{0,4},{4,8},{8,12},{12,0},{1,5},{5,9},{9,13},{13,1},{2,6},{6,10},{... | collective-permute-start | bytes 3145736 | tf_op jit(solution)/shard_map/ppermute | solution.py:17
  24.6 14.2 %collective-permute-start.1 = (bf16[512,1024]{1,0:T(8,128)(2,1)S(1)}, bf16[512,1024]{1,0:T(8,128)(2,1)S(1)}, u32[]{:S(2)}, u32[]{:S(2)}) collective-permute-start(bf16[512,1024]{1,0:T(8,128)(2,1)S(1)} %collective-permute-done), channel_id=1, source_target_pairs={{0,4},{4,8},{8,12},{12,0},{1,5},{5,9},{9,13},{13,1},{2,6},{6,10},{... | collective-permute-start | bytes 3145736 | tf_op jit(solution)/shard_map/ppermute | solution.py:17
  24.7 267.6 %reduce-scatter.2.cloned.1.call-start = ((), (), s32[]{:S(2)}) async-start(), calls=%async_computation.5 | async-start | bytes 5242880 | tf_op jit(solution)/shard_map/reduce_scatter | solution.py:133
  38.8 14.3 %collective-permute-start.2 = (bf16[512,1024]{1,0:T(8,128)(2,1)S(1)}, bf16[512,1024]{1,0:T(8,128)(2,1)}, u32[]{:S(2)}, u32[]{:S(2)}) collective-permute-start(bf16[512,1024]{1,0:T(8,128)(2,1)S(1)} %collective-permute-done.1), channel_id=1, source_target_pairs={{0,4},{4,8},{8,12},{12,0},{1,5},{5,9},{9,13},{13,1},{2,6},{6,10},{... | collective-permute-start | bytes 3145736 | tf_op jit(solution)/shard_map/ppermute | solution.py:17
  56.2 4.4 %copy-start.6 = (f32[4096]{0:T(1024)S(1)}, f32[4096]{0:T(1024)}, u32[]{:S(2)}) copy-start(f32[4096]{0:T(1024)} %param.10) | copy-start | bytes 49156
  56.4 3.2 copy-start.1
  98.4 0.7 copy-start.4
  99.8 80.3 %collective-permute-start.3 = (bf16[2,512,128]{1,2,0:T(8,128)(2,1)}, bf16[2,512,128]{1,2,0:T(8,128)(2,1)}, u32[]{:S(2)}, u32[]{:S(2)}) collective-permute-start(bf16[2,512,128]{1,2,0:T(8,128)(2,1)} %pad_maximum_fusion.1), channel_id=1, source_target_pairs={{0,16},{16,0},{1,17},{17,1},{2,18},{18,2},{3,19},{19,3},{4,20},{20... | collective-permute-start | bytes 786440 | tf_op jit(solution)/shard_map/while/body/eval_jaxpr/ppermute | solution.py:25
  180.1 2.2 copy-start.2
  182.3 2.3 copy-start.5
  249.6 42.8 %copy-start.3 = (bf16[1,512,1024]{2,1,0:T(8,128)(2,1)S(1)}, bf16[1,512,1024]{2,1,0:T(8,128)(2,1)}, u32[]{:S(2)}) copy-start(bf16[1,512,1024]{2,1,0:T(8,128)(2,1)} %param.9) | copy-start | bytes 3145732
Sparse Core Ops, SparseCore 0:
  10.1 42.9 all-gather.4
  55.3 38.9 all-gather.8
  96.4 71.5 all-gather.6
  169.9 73.1 all-gather.10
  249.7 42.5 reduce-scatter.1
